TPU v7x, 256 devices: a whole 4x4x8 slice. The times are simulated.
256 devices in a mesh: section: 4 (over x), mesh: 64 (over z, y, core).
Axes of the slice: x: 4, y: 4, z: 8, core: 2. Of those that a mesh axis runs over, the one named last changes fastest.
Arguments:
- video_tokens: bfloat16 [2, 128, 6144], P(None, 'mesh'), may hold values from -6 to 6
- norm_gain: float32 [4, 6144], P('section'), may hold values from 0.5 to 2
- qkv_weight: bfloat16 [4, 6144, 18432], P('section', None, 'mesh'), may hold values from -0.078125 to 0.078125
- out_weight: bfloat16 [4, 6144, 6144], P('section', 'mesh'), may hold values from -0.078125 to 0.078125
Outputs:
- final_tokens: float32 [2, 128, 6144], P(None, 'mesh', 'section')
All inputs are finite; a program needn't handle non-finite values.
Results may differ from a plain program's by a relative error of at most 0.023.
Values may be sent and summed in bfloat16 or wider, within the bound.
A program may use at most 64 MiB of HBM per device.

v0:
```python
import jax
import jax.numpy as jnp
from jax import lax
from jax.sharding import PartitionSpec as P

HEAD_DIM = 96
PATCHES = 64


epsilon = 1e-06


def laid_out(parts, dim):
    shape = list(parts.shape[1:])
    shape[dim] *= parts.shape[0]
    return jnp.moveaxis(parts, 0, dim).reshape(shape)


def from_everyone(value, axis):
    copies = jnp.broadcast_to(value, (lax.axis_size(axis), *value.shape))
    return lax.all_to_all(copies, axis, split_axis=0, concat_axis=0, tiled=True)


def gathered_copies(value, axis, dim):
    return laid_out(from_everyone(value, axis), dim)


def passed_along(block, axis, distance):
    devices = range(lax.axis_size(axis))
    route = [(i - distance, i) for i in devices if i - distance in devices]
    return lax.ppermute(block, axis, route)


def picked(value, axis, root):
    return lax.dynamic_index_in_dim(lax.all_gather(value, axis), root, 0, keepdims=False)


def build_mask(tokens):
    row_ids = jnp.arange(tokens, dtype=jnp.int32)
    same_frame = row_ids[:, None] // PATCHES == row_ids[None, :] // PATCHES
    same_patch = row_ids[:, None] % PATCHES == row_ids[None, :] % PATCHES
    parity = lax.axis_index("section") % 2
    return jnp.where(parity == 0, same_frame, same_patch)


def section_layer(residual, gain_row, packed_weight, out_columns):
    mean_square = jnp.mean(residual * residual, axis=-1, keepdims=True)
    normed = (residual * lax.rsqrt(mean_square + epsilon) * gain_row[None, :]).astype(jnp.bfloat16)
    packed = jnp.dot(
        gathered_copies(normed, "mesh", 0), packed_weight, preferred_element_type=jnp.float32
    ).astype(jnp.bfloat16)
    tokens = packed.shape[0]
    heads_here = packed.shape[1] // (3 * HEAD_DIM)
    packed = packed.reshape(tokens, heads_here, 3, HEAD_DIM)
    attend_mask = build_mask(tokens)
    scores = jnp.einsum(
        "thd,shd->hts", packed[:, :, 0], packed[:, :, 1], preferred_element_type=jnp.float32
    )
    scores = jnp.where(attend_mask[None], scores * HEAD_DIM ** (-0.5), -1e30)
    weights = jax.nn.softmax(scores, axis=-1).astype(jnp.bfloat16)
    attended = jnp.einsum(
        "hts,shd->thd", weights, packed[:, :, 2], preferred_element_type=jnp.float32
    )
    attended = attended.astype(jnp.bfloat16).reshape(tokens, heads_here * HEAD_DIM)
    summed = jnp.dot(
        gathered_copies(attended, "mesh", 1), out_columns, preferred_element_type=jnp.float32
    )
    projected = lax.all_to_all(
        summed.astype(jnp.bfloat16), "mesh", split_axis=0, concat_axis=1, tiled=True
    ).astype(summed.dtype)
    return residual + projected


def per_device(video_tokens, norm_gain, qkv_weight, out_weight):
    section_count = lax.axis_size("section")
    section_index = lax.axis_index("section")
    gain_row = norm_gain[0]
    packed_weight = qkv_weight[0]
    out_rows = out_weight[0]
    out_columns = lax.all_to_all(out_rows, "mesh", split_axis=1, concat_axis=0, tiled=True)
    micro_count = video_tokens.shape[0]
    carried = jnp.zeros(video_tokens.shape[1:], jnp.float32)
    results = []
    for moment in range(micro_count + section_count - 1):
        incoming = (
            video_tokens[moment].astype(jnp.float32)
            if moment < micro_count
            else jnp.zeros_like(carried)
        )
        current = jnp.where(section_index == 0, incoming, carried)
        produced = section_layer(current, gain_row, packed_weight, out_columns)
        if moment >= section_count - 1:
            results.append(produced)
        if moment < micro_count + section_count - 2:
            carried = passed_along(produced.astype(jnp.bfloat16), "section", 1).astype(
                produced.dtype
            )
    finished = picked(jnp.stack(results).astype(jnp.bfloat16), "section", section_count - 1).astype(
        jnp.float32
    )
    quarter = finished.shape[2] // section_count
    return lax.dynamic_slice_in_dim(finished, section_index * quarter, quarter, 2)


def solution(mesh):
    return jax.shard_map(
        per_device,
        mesh=mesh,
        in_specs=(
            P(None, "mesh", None),
            P("section", None),
            P("section", None, "mesh"),
            P("section", "mesh", None),
        ),
        out_specs=P(None, "mesh", "section"),
        check_vma=False,
    )
```

profile of v0, /device:TPU:1, one launch (start us, length us, event | category | flops | bytes accessed | tf_op | source)
XLA Modules:
  0.0 694.1 jit_solution(10985138959633334154)
XLA Ops:
  3.9 13.3 %all-to-all-start = ((bf16[64,2,6144]{2,1,0:T(2,128)(2,1)}), bf16[64,2,6144]{2,1,0:T(2,128)(2,1)}, u32[]{:S(2)}, u32[]{:S(2)}) async-start(bf16[64,2,6144]{2,1,0:T(2,128)(2,1)} %broadcast_in_dim.28), calls=%async_computation | async-start | bytes 3145728 | tf_op jit(solution)/shard_map/all_to_all | solution.py:21
  19.7 36.5 %all-to-all-done = bf16[64,2,6144]{2,1,0:T(2,128)(2,1)} async-done(((bf16[64,2,6144]{2,1,0:T(2,128)(2,1)}), bf16[64,2,6144]{2,1,0:T(2,128)(2,1)}, u32[]{:S(2)}, u32[]{:S(2)}) %all-to-all-start) | async-done | bytes 1572896 | tf_op jit(solution)/shard_map/all_to_all | solution.py:21
  56.2 6.5 all-to-all-start.2
  62.8 4.5 reshape.429
  70.8 30.9 %all-to-all-done.2 = bf16[96,64,96]{0,2,1:T(8,128)(2,1)} async-done(((bf16[96,64,96]{0,2,1:T(8,128)(2,1)}), bf16[96,64,96]{0,2,1:T(8,128)(2,1)}, u32[]{:S(2)}, u32[]{:S(2)}) %all-to-all-start.2) | async-done | bytes 1179680 | tf_op jit(solution)/shard_map/all_to_all | solution.py:80
  102.7 45.2 %all_to_all.131 = bf16[64,128,96]{1,2,0:T(8,128)(2,1)S(1)} all-to-all(bf16[64,128,96]{1,2,0:T(8,128)(2,1)S(1)} %broadcast_in_dim.30), channel_id=1, replica_groups=mesh['section'=4,'mesh'=64] {'mesh'}, dimensions={0} | all-to-all | bytes 3145728 | tf_op jit(solution)/shard_map/all_to_all | solution.py:21
  147.9 2.6 fusion.90
  151.9 15.8 %all_to_all.132 = bf16[64,2,96]{2,1,0:T(2,128)(2,1)S(1)} all-to-all(bf16[64,2,96]{2,1,0:T(2,128)(2,1)} %bitcast.258), channel_id=1, replica_groups=mesh['section'=4,'mesh'=64] {'mesh'}, dimensions={0} | all-to-all | bytes 49152 | tf_op jit(solution)/shard_map/all_to_all | solution.py:68
  170.8 3.1 collective-permute-start
  177.4 44.8 %all_to_all.133 = bf16[64,2,6144]{2,1,0:T(2,128)(2,1)} all-to-all(bf16[64,2,6144]{2,1,0:T(2,128)(2,1)S(1)} %broadcast_in_dim.31), channel_id=1, replica_groups=mesh['section'=4,'mesh'=64] {'mesh'}, dimensions={0} | all-to-all | bytes 3145728 | tf_op jit(solution)/shard_map/all_to_all | solution.py:21
  222.2 4.5 reshape.435
  229.8 45.3 %all_to_all.134 = bf16[64,128,96]{1,2,0:T(8,128)(2,1)S(1)} all-to-all(bf16[64,128,96]{1,2,0:T(8,128)(2,1)S(1)} %broadcast_in_dim.32), channel_id=1, replica_groups=mesh['section'=4,'mesh'=64] {'mesh'}, dimensions={0} | all-to-all | bytes 3145728 | tf_op jit(solution)/shard_map/all_to_all | solution.py:21
  275.1 2.6 fusion.85
  279.1 15.8 %all_to_all.135 = bf16[64,2,96]{2,1,0:T(2,128)(2,1)S(1)} all-to-all(bf16[64,2,96]{2,1,0:T(2,128)(2,1)} %bitcast.259), channel_id=1, replica_groups=mesh['section'=4,'mesh'=64] {'mesh'}, dimensions={0} | all-to-all | bytes 49152 | tf_op jit(solution)/shard_map/all_to_all | solution.py:68
  298.0 3.9 collective-permute-start.1
  305.1 44.6 %all_to_all.136 = bf16[64,2,6144]{2,1,0:T(2,128)(2,1)} all-to-all(bf16[64,2,6144]{2,1,0:T(2,128)(2,1)S(1)} %broadcast_in_dim.33), channel_id=1, replica_groups=mesh['section'=4,'mesh'=64] {'mesh'}, dimensions={0} | all-to-all | bytes 3145728 | tf_op jit(solution)/shard_map/all_to_all | solution.py:21
  349.7 4.5 reshape.441
  357.3 45.3 %all_to_all.137 = bf16[64,128,96]{1,2,0:T(8,128)(2,1)S(1)} all-to-all(bf16[64,128,96]{1,2,0:T(8,128)(2,1)S(1)} %broadcast_in_dim.34), channel_id=1, replica_groups=mesh['section'=4,'mesh'=64] {'mesh'}, dimensions={0} | all-to-all | bytes 3145728 | tf_op jit(solution)/shard_map/all_to_all | solution.py:21
  402.6 2.6 fusion.80
  406.6 16.0 %all_to_all.138 = bf16[64,2,96]{2,1,0:T(2,128)(2,1)S(1)} all-to-all(bf16[64,2,96]{2,1,0:T(2,128)(2,1)} %bitcast.260), channel_id=1, replica_groups=mesh['section'=4,'mesh'=64] {'mesh'}, dimensions={0} | all-to-all | bytes 49152 | tf_op jit(solution)/shard_map/all_to_all | solution.py:68
  425.7 3.9 collective-permute-start.2
  432.8 44.6 %all_to_all.139 = bf16[64,2,6144]{2,1,0:T(2,128)(2,1)} all-to-all(bf16[64,2,6144]{2,1,0:T(2,128)(2,1)S(1)} %broadcast_in_dim.35), channel_id=1, replica_groups=mesh['section'=4,'mesh'=64] {'mesh'}, dimensions={0} | all-to-all | bytes 3145728 | tf_op jit(solution)/shard_map/all_to_all | solution.py:21
  477.4 4.5 reshape.447
  485.0 45.3 %all_to_all.140 = bf16[64,128,96]{1,2,0:T(8,128)(2,1)S(1)} all-to-all(bf16[64,128,96]{1,2,0:T(8,128)(2,1)S(1)} %broadcast_in_dim.36), channel_id=1, replica_groups=mesh['section'=4,'mesh'=64] {'mesh'}, dimensions={0} | all-to-all | bytes 3145728 | tf_op jit(solution)/shard_map/all_to_all | solution.py:21
  534.3 15.8 %all_to_all.141 = bf16[64,2,96]{2,1,0:T(2,128)(2,1)S(1)} all-to-all(bf16[64,2,96]{2,1,0:T(2,128)(2,1)} %bitcast.261), channel_id=1, replica_groups=mesh['section'=4,'mesh'=64] {'mesh'}, dimensions={0} | all-to-all | bytes 49152 | tf_op jit(solution)/shard_map/all_to_all | solution.py:68
  553.1 3.9 collective-permute-start.3
  560.3 44.8 %all_to_all.142 = bf16[64,2,6144]{2,1,0:T(2,128)(2,1)} all-to-all(bf16[64,2,6144]{2,1,0:T(2,128)(2,1)S(1)} %broadcast_in_dim.37), channel_id=1, replica_groups=mesh['section'=4,'mesh'=64] {'mesh'}, dimensions={0} | all-to-all | bytes 3145728 | tf_op jit(solution)/shard_map/all_to_all | solution.py:21
  605.1 4.5 reshape.453
  612.7 45.3 %all_to_all.143 = bf16[64,128,96]{1,2,0:T(8,128)(2,1)S(1)} all-to-all(bf16[64,128,96]{1,2,0:T(8,128)(2,1)S(1)} %broadcast_in_dim.38), channel_id=1, replica_groups=mesh['section'=4,'mesh'=64] {'mesh'}, dimensions={0} | all-to-all | bytes 3145728 | tf_op jit(solution)/shard_map/all_to_all | solution.py:21
  662.0 6.6 all-to-all-start.15
  668.6 9.4 %all-to-all-done.15 = bf16[64,2,96]{2,1,0:T(2,128)(2,1)} async-done(((bf16[64,2,96]{2,1,0:T(2,128)(2,1)}), bf16[64,2,96]{2,1,0:T(2,128)(2,1)}, u32[]{:S(2)}, u32[]{:S(2)}) %all-to-all-start.15) | async-done | bytes 24608 | tf_op jit(solution)/shard_map/all_to_all | solution.py:68
  682.6 10.4 %all_gather.4 = bf16[4,2,2,6144]{3,2,1,0:T(2,128)(2,1)S(1)} all-gather(bf16[1,2,2,6144]{3,2,1,0:T(2,128)(2,1)S(1)} %pad_maximum_fusion), channel_id=1, replica_groups=mesh['section'=4,'mesh'=64] {'section'}, dimensions={0}, use_global_device_ids=true | all-gather | bytes 245760 | tf_op jit(solution)/shard_map/all_gather | solution.py:35
  (93 shorter events, 66.2 us)
Async XLA Ops:
  0.0 67.3 %copy-start = (bf16[1,6144,288]{1,2,0:T(8,128)(2,1)S(1)}, bf16[1,6144,288]{1,2,0:T(8,128)(2,1)}, u32[]{:S(2)}) copy-start(bf16[1,6144,288]{1,2,0:T(8,128)(2,1)} %param.6) | copy-start | bytes 10616836
  3.9 52.3 %all-to-all-start = ((bf16[64,2,6144]{2,1,0:T(2,128)(2,1)}), bf16[64,2,6144]{2,1,0:T(2,128)(2,1)}, u32[]{:S(2)}, u32[]{:S(2)}) async-start(bf16[64,2,6144]{2,1,0:T(2,128)(2,1)} %broadcast_in_dim.28), calls=%async_computation | async-start | bytes 3145728 | tf_op jit(solution)/shard_map/all_to_all | solution.py:21
  56.2 45.5 %all-to-all-start.2 = ((bf16[96,64,96]{0,2,1:T(8,128)(2,1)}), bf16[96,64,96]{0,2,1:T(8,128)(2,1)}, u32[]{:S(2)}, u32[]{:S(2)}) async-start(bf16[96,64,96]{0,2,1:T(8,128)(2,1)} %bitcast.251), calls=%async_computation.2 | async-start | bytes 3145728 | tf_op jit(solution)/shard_map/all_to_all | solution.py:80
  170.8 4.1 collective-permute-start
  174.8 0.9 copy-start.4
  298.0 4.9 collective-permute-start.1
  302.9 0.6 copy-start.2
  425.7 4.9 collective-permute-start.2
  430.5 0.6 copy-start.3
  553.1 5.1 copy-start.5
  553.1 4.9 collective-permute-start.3
  558.0 0.6 copy-start.1
  662.0 16.0 %all-to-all-start.15 = ((bf16[64,2,96]{2,1,0:T(2,128)(2,1)}), bf16[64,2,96]{2,1,0:T(2,128)(2,1)}, u32[]{:S(2)}, u32[]{:S(2)}) async-start(bf16[64,2,96]{2,1,0:T(2,128)(2,1)} %bitcast.257), calls=%async_computation.15 | async-start | bytes 65536 | tf_op jit(solution)/shard_map/all_to_all | solution.py:68
where the time goes:
time: 706 us; the launch traced here: 694 us
  blocking collectives  479 us (68%)
  waiting for transfers between devices  80.5 us (11%)
  local copies, waits for them, and re-layouts  51.6 us (7%)
  starting transfers between devices  41.3 us (6%)
  matrix products  27.7 us (4%)
  other arithmetic  13.4 us (2%)
    all_to_all x9, blocking collectives, from_everyone(): return lax.all_to_all(copies, axis, split_axis=0, concat_axis=0, tiled=True)  405 us
    all_to_all x4, blocking collectives, section_layer(): lax.all_to_all(summed.astype(jnp.bfloat16), 'mesh', split_axis=0, concat_...  63.4 us
    all_to_all x1, waiting for transfers between devices, from_everyone(): return lax.all_to_all(copies, axis, split_axis=0, concat_axis=0, tiled=True)  36.5 us
    all_to_all x1, waiting for transfers between devices, per_device(): lax.all_to_all(out_rows, 'mesh', split_axis=1, concat_axis=0, tiled=True)  30.9 us
    reshape x5, local copies, waits for them, and re-layouts, laid_out(): return jnp.moveaxis(parts, 0, dim).reshape(shape)  22.5 us
    ppermute x4, starting transfers between devices, passed_along(): return lax.ppermute(block, axis, route)  14.9 us
  transfers between devices with their start and end apart: 7, of which 7 were waited for; matrix products, arithmetic and copies ran while one was open for 2% of the time, Pallas kernels for 0%

commit v1 on v0

v1 whole, which is shorter than its diff:
```python
import jax
import jax.numpy as jnp
from jax import lax
from jax.experimental import pallas as pl
from jax.experimental.pallas import tpu as pltpu
from jax.sharding import PartitionSpec as P

MESH = pl.DeviceIdType.MESH
HEAD = 96
PAD = 128
Z, Y, G = 8, 4, 8
ROWS = 16
WIDE = 768
TOKENS = 128
D = 6144
LAST = 3
EPS = 1e-06
ORDER = (0, 1, 7, 2, 6, 3, 5, 4)
BF = jnp.bfloat16
F32 = jnp.float32


def kernel(
    tok_ref, gain_ref, w_hbm, wo_hbm, out_ref,
    x, wraw, wp, wo, acc, ssq, att, part, rsb, slab, fin, ini_s, ini_r,
    wsem, ini_ss, ini_rs, wo_ss, wo_rs, wo_ls, zi_ss, z_ss, z_rs, y_ss, y_rs, r_ss, r_rs,
    d_ss, d_rs, a_ss, a_rs, p_ss, p_rs, f_ss, f_rs,
):
    s = lax.axis_index("section")
    me = lax.axis_index("mesh")
    z, j = me // G, me % G
    y, c = j // 2, j % 2

    def at(sec, zz, jj):
        return (sec, zz * G + jj)

    def send(src, dst, ssem, rsem, dev):
        pltpu.make_async_remote_copy(
            src_ref=src, dst_ref=dst, send_sem=ssem, recv_sem=rsem, device_id=dev, device_id_type=MESH
        ).start()

    def drain(ref, sem):
        pltpu.make_async_copy(ref, ref, sem).wait()

    def rows(zz):
        return pl.ds(pl.multiple_of(zz * ROWS, ROWS), ROWS)

    def other(jj, k):
        return (jj + k) % G

    wcopy = pltpu.make_async_copy(w_hbm, wraw, wsem)
    wcopy.start()
    own_wo = pltpu.make_async_copy(
        wo_hbm.at[:, pl.ds(pl.multiple_of(j * WIDE, WIDE), WIDE)], wo.at[j, pl.ds(0, HEAD)], wo_ls
    )
    own_wo.start()

    barrier = pltpu.get_barrier_semaphore()

    def greet(dev):
        pl.semaphore_signal(barrier, inc=1, device_id=dev, device_id_type=MESH)

    for k in range(1, G):
        greet(at(s, z, other(j, k)))
    for k in range(1, Z):
        greet(at(s, (z + k) % Z, j))

    @pl.when(s < LAST)
    def _():
        for k in range(Z):
            greet(at(s + 1, k, j))
        for k in range(2):
            greet(at(LAST, z, 2 * s + k))

    @pl.when(s > 0)
    def _():
        for k in range(Z):
            greet(at(s - 1, k, j))

    @pl.when(jnp.logical_and(s == LAST, y < LAST))
    def _():
        for k in range(G):
            greet(at(y, z, k))

    greeted = G - 1 + Z - 1 + jnp.where(s < LAST, Z + 2, 0) + jnp.where(s > 0, Z, 0)
    pl.semaphore_wait(barrier, greeted + jnp.where(jnp.logical_and(s == LAST, y < LAST), G, 0))

    @pl.when(s == 0)
    def _():
        for g in range(G):
            for m in range(2):
                ini_s[g, m] = tok_ref[m, :, g * WIDE:(g + 1) * WIDE].astype(F32)
        for k in range(1, G):
            to = other(j, k)
            send(ini_s.at[to], ini_r.at[j], ini_ss, ini_rs, at(s, z, to))

    for k in range(1, G):
        to = other(j, k)
        send(
            wo_hbm.at[:, pl.ds(pl.multiple_of(to * WIDE, WIDE), WIDE)], wo.at[j, pl.ds(0, HEAD)],
            wo_ss, wo_rs, at(s, z, to),
        )
    for g in range(G):
        wo[g, HEAD:PAD, :] = jnp.zeros((PAD - HEAD, WIDE), BF)

    wcopy.wait()

    def prepare(g, carry):
        for i in range(WIDE // 128):
            at_row = pl.multiple_of(g * WIDE + i * 128, 128)
            gain = jnp.broadcast_to(gain_ref[:, pl.ds(at_row, 128)], (128, 128)).T[:, :HEAD]
            w = wraw[pl.ds(at_row, 128), :].astype(F32)
            blank = jnp.zeros((128, PAD - HEAD), F32)
            for q in range(3):
                piece = w[:, q * HEAD:(q + 1) * HEAD] * gain
                wp[g, i * 128:(i + 1) * 128, q * PAD:(q + 1) * PAD] = jnp.concatenate([piece, blank], axis=1).astype(BF)
        return carry

    lax.fori_loop(0, G, prepare, 0)

    def spread(src, m, sec, ssem, skip_own):
        for d in ORDER:
            if d == 0 and skip_own:
                continue
            send(src, x.at[m, j, rows(z)], ssem, z_rs.at[m, z], at(sec, (z + d) % Z, j))

    @pl.when(s == 0)
    def _():
        ini_r[j] = ini_s[j]
        drain(ini_r.at[pl.ds(0, G - 1)], ini_rs)
        for m in range(2):
            whole = jnp.concatenate([ini_r[g, m] for g in range(G)], axis=0).astype(BF)
            slab[m] = whole
            x[m, j, rows(z), :] = whole
            spread(slab.at[m], m, s, zi_ss.at[m], True)

    def take_rows(m):
        for i, d in enumerate(ORDER):
            zz = (z + d) % Z
            chunk = x.at[m, j, rows(zz)]
            if d == 0:
                @pl.when(s > 0)
                def _():
                    drain(chunk, z_rs.at[m, zz])
            else:
                drain(chunk, z_rs.at[m, zz])
            half = 0 if i < 4 else 1
            send(chunk, chunk, y_ss.at[m], y_rs.at[m, 0, half], at(s, z, other(j, 2)))
            send(chunk, chunk, y_ss.at[m], y_rs.at[m, 1, half], at(s, z, other(j, 6)))
        share(m, 0, j)

    def sibling(jj):
        return jj + 1 - 2 * c

    def share(m, slot, jj):
        send(x.at[m, jj], x.at[m, jj], d_ss.at[m], d_rs.at[m, slot], at(s, z, sibling(j)))

    def multiply(m, jj, first=False):
        xs = x[m, jj]
        wide = xs.astype(F32)
        squares = wide * wide
        total = squares[:, :128]
        for i in range(1, WIDE // 128):
            total += squares[:, i * 128:(i + 1) * 128]
        product = jnp.dot(xs, wp[jj], preferred_element_type=F32)
        if first:
            acc[m] = product
            ssq[m] = total
        else:
            acc[m] += product
            ssq[m] += total

    def relay(m, jj, half, to, slot):
        for d in ORDER[half * 4:half * 4 + 4]:
            chunk = x.at[m, jj, rows((z + d) % Z)]
            send(chunk, chunk, r_ss.at[m], r_rs.at[m, slot], at(s, z, to))

    def take_groups(m):
        before, after, across = other(j, 6), other(j, 2), other(j, 4)
        half_rows = pl.ds(0, TOKENS // 2)
        multiply(m, j, True)
        drain(x.at[m, before, half_rows], y_rs.at[m, 0, 0])
        relay(m, before, 0, after, 0)
        drain(x.at[m, after, half_rows], y_rs.at[m, 1, 0])
        drain(x.at[m, after, half_rows], y_rs.at[m, 1, 1])
        relay(m, after, 1, before, 1)
        share(m, 1, after)
        drain(x.at[m, before, half_rows], y_rs.at[m, 0, 1])
        share(m, 2, before)
        multiply(m, after)
        multiply(m, before)
        drain(x.at[m, j], d_rs.at[m, 0])
        multiply(m, sibling(j))
        drain(x.at[m, across, half_rows], r_rs.at[m, 0])
        drain(x.at[m, across, half_rows], r_rs.at[m, 1])
        share(m, 3, across)
        multiply(m, across)
        for slot, jj in ((1, after), (2, before), (3, across)):
            drain(x.at[m, jj], d_rs.at[m, slot])
            multiply(m, sibling(jj))

    def attend(m):
        mean = jnp.sum(ssq[m], axis=-1, keepdims=True) * (1.0 / D)
        packed = (acc[m] * lax.rsqrt(mean + EPS)).astype(BF)
        q, k, v = packed[:, :PAD], packed[:, PAD:2 * PAD], packed[:, 2 * PAD:]
        scores = lax.dot_general(q, k, (((1,), (1,)), ((), ())), preferred_element_type=F32)
        t = lax.broadcasted_iota(jnp.int32, (TOKENS, TOKENS), 0)
        u = lax.broadcasted_iota(jnp.int32, (TOKENS, TOKENS), 1)
        bits = jnp.where(s % 2 == 0, 64, 63)
        scores = jnp.where(((t ^ u) & bits) == 0, scores * HEAD ** (-0.5), -1e30)
        top = jnp.max(scores, axis=-1, keepdims=True)
        e = jnp.exp(scores - top)
        weights = (e / jnp.sum(e, axis=-1, keepdims=True)).astype(BF)
        att[m, j] = jnp.dot(weights, v, preferred_element_type=F32).astype(BF)
        for k in (4, 2, 6, 3, 5, 1, 7):
            send(att.at[m, j], att.at[m, j], a_ss.at[m], a_rs.at[m], at(s, z, other(j, k)))

    def project(m):
        drain(att.at[m, pl.ds(0, G - 1)], a_rs.at[m])
        together = jnp.concatenate([att[m, g] for g in range(G)], axis=1)
        part[m] = jnp.dot(together, wo[...].reshape(G * PAD, WIDE), preferred_element_type=F32).astype(BF)
        for d in ORDER[::-1][:-1]:
            zz = (z + d) % Z
            send(part.at[m, rows(zz)], rsb.at[m, z], p_ss.at[m], p_rs.at[m], at(s, zz, j))

    def finish(m):
        total = x[m, j, rows(z), :].astype(F32) + part[m, rows(z), :].astype(F32)
        drain(rsb.at[m, pl.ds(0, Z - 1)], p_rs.at[m])
        for d in range(1, Z):
            total += rsb[m, (z + d) % Z].astype(F32)

        @pl.when(s < LAST)
        def _():
            slab[2 + m] = total.astype(BF)
            spread(slab.at[2 + m], m, s + 1, z_ss.at[m], False)

        @pl.when(s == LAST)
        def _():
            for g in range(G):
                fin[m, g] = total[2 * g:2 * g + 2, :]
            columns = pl.ds(pl.multiple_of(c * WIDE, WIDE), WIDE)

            @pl.when(y < LAST)
            def _():
                for g in range(G):
                    send(fin.at[m, g], out_ref.at[m, :, columns], f_ss.at[m], f_rs.at[m, c], at(y, z, g))

            @pl.when(y == LAST)
            def _():
                out_ref[m, :, columns] = fin[m, j]
                for k in range(1, G):
                    to = other(j, k)
                    send(fin.at[m, to], out_ref.at[m, :, columns], f_ss.at[m], f_rs.at[m, c], at(s, z, to))

    take_rows(0)
    take_rows(1)
    take_groups(0)
    attend(0)
    own_wo.wait()
    drain(wo.at[pl.ds(0, G - 1), pl.ds(0, HEAD)], wo_rs)
    project(0)
    take_groups(1)
    attend(1)
    finish(0)
    project(1)
    finish(1)

    drain(wo.at[pl.ds(0, G - 1), pl.ds(0, HEAD)], wo_ss)

    @pl.when(s == 0)
    def _():
        drain(ini_s.at[pl.ds(0, G - 1)], ini_ss)
        for m in range(2):
            drain(x.at[m, 0, pl.ds(0, TOKENS - ROWS)], zi_ss.at[m])

    for m in range(2):
        drain(x.at[m, pl.ds(0, 2)], y_ss.at[m])
        drain(x.at[m, 0], r_ss.at[m])
        drain(x.at[m, pl.ds(0, 4)], d_ss.at[m])
        drain(att.at[m, pl.ds(0, G - 1)], a_ss.at[m])
        drain(rsb.at[m, pl.ds(0, Z - 1)], p_ss.at[m])

        @pl.when(s < LAST)
        def _():
            drain(x.at[m, 0], z_ss.at[m])

        @pl.when(jnp.logical_and(s == LAST, y < LAST))
        def _():
            drain(fin.at[m], f_ss.at[m])

        @pl.when(jnp.logical_and(s == LAST, y == LAST))
        def _():
            drain(fin.at[m, pl.ds(0, G - 1)], f_ss.at[m])

        for k in range(2):
            @pl.when(jnp.logical_not(jnp.logical_and(s == LAST, jnp.logical_and(y == LAST, c == k))))
            def _():
                drain(out_ref.at[m, :, pl.ds(k * WIDE, WIDE)], f_rs.at[m, k])


def per_device(video_tokens, norm_gain, qkv_weight, out_weight):
    vmem = pl.BlockSpec(memory_space=pltpu.VMEM)
    anywhere = pl.BlockSpec(memory_space=pl.ANY)
    dma = pltpu.SemaphoreType.DMA
    return pl.pallas_call(
        kernel,
        out_shape=jax.ShapeDtypeStruct((2, 2, 2 * WIDE), F32),
        in_specs=[vmem, vmem, anywhere, anywhere],
        out_specs=vmem,
        scratch_shapes=[
            pltpu.VMEM((2, G, TOKENS, WIDE), BF),
            pltpu.VMEM((D, 3 * HEAD), BF),
            pltpu.VMEM((G, WIDE, 3 * PAD), BF),
            pltpu.VMEM((G, PAD, WIDE), BF),
            pltpu.VMEM((2, TOKENS, 3 * PAD), F32),
            pltpu.VMEM((2, TOKENS, 128), F32),
            pltpu.VMEM((2, G, TOKENS, PAD), BF),
            pltpu.VMEM((2, TOKENS, WIDE), BF),
            pltpu.VMEM((2, Z, ROWS, WIDE), BF),
            pltpu.VMEM((4, ROWS, WIDE), BF),
            pltpu.VMEM((2, G, 2, WIDE), F32),
            pltpu.VMEM((G, 2, 2, WIDE), F32),
            pltpu.VMEM((G, 2, 2, WIDE), F32),
            dma, dma, dma, dma, dma, dma, dma((2,)), dma((2,)), dma((2, Z)), dma((2,)), dma((2, 2, 2)),
            dma((2,)), dma((2, 2)), dma((2,)), dma((2, 4)), dma((2,)), dma((2,)), dma((2,)), dma((2,)),
            dma((2,)), dma((2, 2)),
        ],
        compiler_params=pltpu.CompilerParams(
            collective_id=0, has_side_effects=True, vmem_limit_bytes=56 * 1024 * 1024
        ),
    )(video_tokens, norm_gain, qkv_weight[0], out_weight[0])


def solution(mesh):
    return jax.shard_map(
        per_device,
        mesh=mesh,
        in_specs=(
            P(None, "mesh", None),
            P("section", None),
            P("section", None, "mesh"),
            P("section", "mesh", None),
        ),
        out_specs=P(None, "mesh", "section"),
        check_vma=False,
    )
```

time: 706 us -> 196 us (0.28); the launches traced: 694 us -> 195 us
  blocking collectives: 479 us -> 0 us
  Pallas kernels: 0 us -> 188 us
  waiting for transfers between devices: 80.5 us -> 0 us
  local copies, waits for them, and re-layouts: 51.6 us -> 7.61 us
  starting transfers between devices: 41.3 us -> 0 us
  matrix products: 27.7 us -> 0 us
  other arithmetic: 13.4 us -> 0 us
    all_to_all x13 -> x0, blocking collectives: 468 us -> none  [the longest x9 405 us: from_everyone(): return lax.all_to_all(copies, axis, split_axis=0, concat_axis=0, tiled=True)]
    pallas_call x0 -> x1, Pallas kernels: none -> 188 us  [per_device(): pl.pallas_call(kernel, out_shape=jax.ShapeDtypeStruct((2, 2, 2 * WIDE), F...]
    all_to_all x3 -> x0, waiting for transfers between devices: 76.8 us -> none  [the longest x1 36.5 us: from_everyone(): return lax.all_to_all(copies, axis, split_axis=0, concat_axis=0, tiled=True)]
    dot_general x20 -> x0, matrix products: 27.7 us -> none  [the longest x5 12.8 us: section_layer(): jnp.dot(gathered_copies(attended, 'mesh', 1), out_columns, preferred_elem...]
    all_to_all x3 -> x0, starting transfers between devices: 26.4 us -> none  [the longest x1 13.3 us: from_everyone(): return lax.all_to_all(copies, axis, split_axis=0, concat_axis=0, tiled=True)]
    reshape x5 -> x0, local copies, waits for them, and re-layouts: 22.5 us -> none  [laid_out(): return jnp.moveaxis(parts, 0, dim).reshape(shape)]
    convert_element_type x15 -> x0, local copies, waits for them, and re-layouts: 18.2 us -> none  [the longest x10 11 us: section_layer(): projected = lax.all_to_all(summed.astype(jnp.bfloat16), 'mesh', split_axi...]
    ppermute x4 -> x0, starting transfers between devices: 14.9 us -> none  [passed_along(): return lax.ppermute(block, axis, route)]
  transfers between devices with their start and end apart: 7 -> 0, of which waited for: 7 -> 0; matrix products, arithmetic and copies ran while one was open for 2% -> 0% of each run, Pallas kernels for 0% -> 0%
where the time goes in v1:
time: 196 us; the launch traced here: 195 us
  Pallas kernels  188 us (96%)
  local copies, waits for them, and re-layouts  7.61 us (4%)
    pallas_call x1, Pallas kernels, per_device(): pl.pallas_call(kernel, out_shape=jax.ShapeDtypeStruct((2, 2, 2 * WIDE), F...  188 us
    unnamed x2, local copies, waits for them, and re-layouts  7.61 us

profile of v1, /device:TPU:1, one launch (start us, length us, event | category | flops | bytes accessed | tf_op | source)
XLA Modules:
  0.0 195.5 jit_solution(368054732490603406)
XLA Ops:
  0.0 6.3 %copy.5 = bf16[1,6144,288]{2,1,0:T(8,128)(2,1)} copy(bf16[1,6144,288]{1,2,0:T(8,128)(2,1)} %param.6) | data formatting | bytes 7077888 | tf_op args[2]
  6.3 187.8 %shard_map.46 = f32[2,2,1536]{2,1,0:T(2,128)} custom-call(bf16[2,2,6144]{2,1,0:T(2,128)(2,1)} %tok_ref.1, f32[1,6144]{1,0:T(1,128)} %gain_ref.1, bf16[6144,288]{1,0:T(8,128)(2,1)} %bitcast.2, bf16[96,6144]{1,0:T(8,128)(2,1)} %bitcast.3), custom_call_target="tpu_custom_call" | custom-call | tf_op jit(solution)/shard_map/pallas_call | solution.py:305
  194.1 1.3 copy.7

commit v2 on v1

--- a/solution.py
+++ b/solution.py
@@ -22,8 +22,8 @@
 
 def kernel(
     tok_ref, gain_ref, w_hbm, wo_hbm, out_ref,
-    x, wraw, wp, wo, acc, ssq, att, part, rsb, slab, fin, ini_s, ini_r,
-    wsem, ini_ss, ini_rs, wo_ss, wo_rs, wo_ls, zi_ss, z_ss, z_rs, y_ss, y_rs, r_ss, r_rs,
+    x, wraw, wp, wo, stage, acc, ssq, att, part, rsb, slab, fin, ini_s, ini_r,
+    wsem, ini_ss, ini_rs, wo_ss, wo_rs, wo_ls, st_ss, st_rs, zi_ss, z_ss, z_rs, y_ss, y_rs, r_rs,
     d_ss, d_rs, a_ss, a_rs, p_ss, p_rs, f_ss, f_rs,
 ):
     s = lax.axis_index("section")
@@ -51,7 +51,7 @@
     wcopy = pltpu.make_async_copy(w_hbm, wraw, wsem)
     wcopy.start()
     own_wo = pltpu.make_async_copy(
-        wo_hbm.at[:, pl.ds(pl.multiple_of(j * WIDE, WIDE), WIDE)], wo.at[j, pl.ds(0, HEAD)], wo_ls
+        wo_hbm.at[:, pl.ds(pl.multiple_of(j * WIDE, WIDE), WIDE)], wo.at[j], wo_ls
     )
     own_wo.start()
 
@@ -82,41 +82,55 @@
         for k in range(G):
             greet(at(y, z, k))
 
-    greeted = G - 1 + Z - 1 + jnp.where(s < LAST, Z + 2, 0) + jnp.where(s > 0, Z, 0)
-    pl.semaphore_wait(barrier, greeted + jnp.where(jnp.logical_and(s == LAST, y < LAST), G, 0))
+    wcopy.wait()
+
+    def prepare(g, carry):
+        features = pl.ds(pl.multiple_of(g * WIDE, WIDE), WIDE)
+        blank = jnp.zeros((PAD - HEAD, WIDE), F32)
+        for q in range(3):
+            piece = wraw[q * HEAD:(q + 1) * HEAD, features].astype(F32) * gain_ref[:, features]
+            wp[g, :, q * PAD:(q + 1) * PAD] = jnp.concatenate([piece, blank], axis=0).T.astype(BF)
+        return carry
+
+    lax.fori_loop(0, G, prepare, 0)
 
     @pl.when(s == 0)
     def _():
         for g in range(G):
             for m in range(2):
                 ini_s[g, m] = tok_ref[m, :, g * WIDE:(g + 1) * WIDE].astype(F32)
+
+    greeted = G - 1 + Z - 1 + jnp.where(s < LAST, Z + 2, 0) + jnp.where(s > 0, Z, 0)
+    pl.semaphore_wait(barrier, greeted + jnp.where(jnp.logical_and(s == LAST, y < LAST), G, 0))
+
+    @pl.when(s == 0)
+    def _():
         for k in range(1, G):
             to = other(j, k)
             send(ini_s.at[to], ini_r.at[j], ini_ss, ini_rs, at(s, z, to))
 
-    for k in range(1, G):
-        to = other(j, k)
-        send(
-            wo_hbm.at[:, pl.ds(pl.multiple_of(to * WIDE, WIDE), WIDE)], wo.at[j, pl.ds(0, HEAD)],
-            wo_ss, wo_rs, at(s, z, to),
-        )
-    for g in range(G):
-        wo[g, HEAD:PAD, :] = jnp.zeros((PAD - HEAD, WIDE), BF)
-
-    wcopy.wait()
-
-    def prepare(g, carry):
-        for i in range(WIDE // 128):
-            at_row = pl.multiple_of(g * WIDE + i * 128, 128)
-            gain = jnp.broadcast_to(gain_ref[:, pl.ds(at_row, 128)], (128, 128)).T[:, :HEAD]
-            w = wraw[pl.ds(at_row, 128), :].astype(F32)
-            blank = jnp.zeros((128, PAD - HEAD), F32)
-            for q in range(3):
-                piece = w[:, q * HEAD:(q + 1) * HEAD] * gain
-                wp[g, i * 128:(i + 1) * 128, q * PAD:(q + 1) * PAD] = jnp.concatenate([piece, blank], axis=1).astype(BF)
-        return carry
-
-    lax.fori_loop(0, G, prepare, 0)
+    def share_wo(dy, cc, to=None, dst=None, rsem=None):
+        goal = (y + dy) % Y * 2 + cc
+        columns = pl.ds(pl.multiple_of(goal * WIDE, WIDE), WIDE)
+        if to is None:
+            to, dst, rsem = goal, wo.at[j], wo_rs
+        send(wo_hbm.at[:, columns], dst, wo_ss, rsem, at(s, z, to))
+
+    share_wo(2, 1 - c, other(j, 6), stage, st_rs)
+    share_wo(0, 1 - c)
+    share_wo(1, c)
+    share_wo(3, c)
+
+    def share_wo_rest():
+        share_wo(2, c)
+        share_wo(1, 1 - c)
+        share_wo(3, 1 - c)
+        drain(stage, st_rs)
+        send(stage, wo.at[other(j, 2)], st_ss, wo_rs, at(s, z, other(j, 6) + 1 - 2 * c))
+
+    @pl.when(s > 0)
+    def _():
+        share_wo_rest()
 
     def spread(src, m, sec, ssem, skip_own):
         for d in ORDER:
@@ -147,6 +161,7 @@
             half = 0 if i < 4 else 1
             send(chunk, chunk, y_ss.at[m], y_rs.at[m, 0, half], at(s, z, other(j, 2)))
             send(chunk, chunk, y_ss.at[m], y_rs.at[m, 1, half], at(s, z, other(j, 6)))
+            send(chunk, chunk, y_ss.at[m], r_rs.at[m, half], at(s, z, other(j, 4)))
         share(m, 0, j)
 
     def sibling(jj):
@@ -170,32 +185,23 @@
             acc[m] += product
             ssq[m] += total
 
-    def relay(m, jj, half, to, slot):
-        for d in ORDER[half * 4:half * 4 + 4]:
-            chunk = x.at[m, jj, rows((z + d) % Z)]
-            send(chunk, chunk, r_ss.at[m], r_rs.at[m, slot], at(s, z, to))
-
     def take_groups(m):
         before, after, across = other(j, 6), other(j, 2), other(j, 4)
         half_rows = pl.ds(0, TOKENS // 2)
         multiply(m, j, True)
-        drain(x.at[m, before, half_rows], y_rs.at[m, 0, 0])
-        relay(m, before, 0, after, 0)
-        drain(x.at[m, after, half_rows], y_rs.at[m, 1, 0])
-        drain(x.at[m, after, half_rows], y_rs.at[m, 1, 1])
-        relay(m, after, 1, before, 1)
+        for half in range(2):
+            drain(x.at[m, after, half_rows], y_rs.at[m, 1, half])
         share(m, 1, after)
-        drain(x.at[m, before, half_rows], y_rs.at[m, 0, 1])
+        for half in range(2):
+            drain(x.at[m, before, half_rows], y_rs.at[m, 0, half])
         share(m, 2, before)
+        for half in range(2):
+            drain(x.at[m, across, half_rows], r_rs.at[m, half])
+        share(m, 3, across)
         multiply(m, after)
         multiply(m, before)
-        drain(x.at[m, j], d_rs.at[m, 0])
-        multiply(m, sibling(j))
-        drain(x.at[m, across, half_rows], r_rs.at[m, 0])
-        drain(x.at[m, across, half_rows], r_rs.at[m, 1])
-        share(m, 3, across)
         multiply(m, across)
-        for slot, jj in ((1, after), (2, before), (3, across)):
+        for slot, jj in ((0, j), (1, after), (2, before), (3, across)):
             drain(x.at[m, jj], d_rs.at[m, slot])
             multiply(m, sibling(jj))
 
@@ -211,14 +217,16 @@
         top = jnp.max(scores, axis=-1, keepdims=True)
         e = jnp.exp(scores - top)
         weights = (e / jnp.sum(e, axis=-1, keepdims=True)).astype(BF)
-        att[m, j] = jnp.dot(weights, v, preferred_element_type=F32).astype(BF)
+        across = lax.dot_general(v, weights, (((0,), (1,)), ((), ())), preferred_element_type=F32)
+        att[m, j] = across[:HEAD].astype(BF)
         for k in (4, 2, 6, 3, 5, 1, 7):
             send(att.at[m, j], att.at[m, j], a_ss.at[m], a_rs.at[m], at(s, z, other(j, k)))
 
     def project(m):
         drain(att.at[m, pl.ds(0, G - 1)], a_rs.at[m])
-        together = jnp.concatenate([att[m, g] for g in range(G)], axis=1)
-        part[m] = jnp.dot(together, wo[...].reshape(G * PAD, WIDE), preferred_element_type=F32).astype(BF)
+        together = att[m].reshape(G * HEAD, TOKENS)
+        product = lax.dot_general(together, wo[...].reshape(G * HEAD, WIDE), (((0,), (0,)), ((), ())), preferred_element_type=F32)
+        part[m] = product.astype(BF)
         for d in ORDER[::-1][:-1]:
             zz = (z + d) % Z
             send(part.at[m, rows(zz)], rsb.at[m, z], p_ss.at[m], p_rs.at[m], at(s, zz, j))
@@ -253,19 +261,25 @@
                     send(fin.at[m, to], out_ref.at[m, :, columns], f_ss.at[m], f_rs.at[m, c], at(s, z, to))
 
     take_rows(0)
-    take_rows(1)
+
+    @pl.when(s == 0)
+    def _():
+        share_wo_rest()
+
     take_groups(0)
     attend(0)
     own_wo.wait()
-    drain(wo.at[pl.ds(0, G - 1), pl.ds(0, HEAD)], wo_rs)
+    drain(wo.at[pl.ds(0, G - 1)], wo_rs)
     project(0)
+    take_rows(1)
+    finish(0)
     take_groups(1)
     attend(1)
-    finish(0)
     project(1)
     finish(1)
 
-    drain(wo.at[pl.ds(0, G - 1), pl.ds(0, HEAD)], wo_ss)
+    drain(wo.at[pl.ds(0, G - 1)], wo_ss)
+    drain(stage, st_ss)
 
     @pl.when(s == 0)
     def _():
@@ -274,8 +288,7 @@
             drain(x.at[m, 0, pl.ds(0, TOKENS - ROWS)], zi_ss.at[m])
 
     for m in range(2):
-        drain(x.at[m, pl.ds(0, 2)], y_ss.at[m])
-        drain(x.at[m, 0], r_ss.at[m])
+        drain(x.at[m, pl.ds(0, 3)], y_ss.at[m])
         drain(x.at[m, pl.ds(0, 4)], d_ss.at[m])
         drain(att.at[m, pl.ds(0, G - 1)], a_ss.at[m])
         drain(rsb.at[m, pl.ds(0, Z - 1)], p_ss.at[m])
@@ -309,26 +322,27 @@
         out_specs=vmem,
         scratch_shapes=[
             pltpu.VMEM((2, G, TOKENS, WIDE), BF),
-            pltpu.VMEM((D, 3 * HEAD), BF),
+            pltpu.VMEM((3 * HEAD, D), BF),
             pltpu.VMEM((G, WIDE, 3 * PAD), BF),
-            pltpu.VMEM((G, PAD, WIDE), BF),
+            pltpu.VMEM((G, HEAD, WIDE), BF),
+            pltpu.VMEM((HEAD, WIDE), BF),
             pltpu.VMEM((2, TOKENS, 3 * PAD), F32),
             pltpu.VMEM((2, TOKENS, 128), F32),
-            pltpu.VMEM((2, G, TOKENS, PAD), BF),
+            pltpu.VMEM((2, G, HEAD, TOKENS), BF),
             pltpu.VMEM((2, TOKENS, WIDE), BF),
             pltpu.VMEM((2, Z, ROWS, WIDE), BF),
             pltpu.VMEM((4, ROWS, WIDE), BF),
             pltpu.VMEM((2, G, 2, WIDE), F32),
             pltpu.VMEM((G, 2, 2, WIDE), F32),
             pltpu.VMEM((G, 2, 2, WIDE), F32),
-            dma, dma, dma, dma, dma, dma, dma((2,)), dma((2,)), dma((2, Z)), dma((2,)), dma((2, 2, 2)),
-            dma((2,)), dma((2, 2)), dma((2,)), dma((2, 4)), dma((2,)), dma((2,)), dma((2,)), dma((2,)),
+            dma, dma, dma, dma, dma, dma, dma, dma, dma((2,)), dma((2,)), dma((2, Z)), dma((2,)), dma((2, 2, 2)),
+            dma((2, 2)), dma((2,)), dma((2, 4)), dma((2,)), dma((2,)), dma((2,)), dma((2,)),
             dma((2,)), dma((2, 2)),
         ],
         compiler_params=pltpu.CompilerParams(
             collective_id=0, has_side_effects=True, vmem_limit_bytes=56 * 1024 * 1024
         ),
-    )(video_tokens, norm_gain, qkv_weight[0], out_weight[0])
+    )(video_tokens, norm_gain, qkv_weight[0].T, out_weight[0])
 
 
 def solution(mesh):

time: 196 us -> 156 us (0.80)
  Pallas kernels: 188 us -> 154 us
  local copies, waits for them, and re-layouts: 7.61 us -> 1.35 us
    pallas_call x1, Pallas kernels: 188 us -> 154 us  [per_device(): pl.pallas_call(kernel, out_shape=jax.ShapeDtypeStruct((2, 2, 2 * WIDE), F...]
    unnamed x2 -> x1, local copies, waits for them, and re-layouts: 7.61 us -> 1.35 us
where the time goes in v2:
time: 156 us; the launch traced here: 155 us
  Pallas kernels  154 us (99%)
    pallas_call x1, Pallas kernels, per_device(): pl.pallas_call(kernel, out_shape=jax.ShapeDtypeStruct((2, 2, 2 * WIDE), F...  154 us

profile of v2, /device:TPU:1, one launch (start us, length us, event | category | flops | bytes accessed | tf_op | source)
XLA Modules:
  0.0 155.4 jit_solution(8429425845425717784)
XLA Ops:
  0.0 154.0 %shard_map.46 = f32[2,2,1536]{2,1,0:T(2,128)} custom-call(bf16[2,2,6144]{2,1,0:T(2,128)(2,1)} %tok_ref.1, f32[1,6144]{1,0:T(1,128)} %gain_ref.1, bf16[288,6144]{1,0:T(8,128)(2,1)} %bitcast.4, bf16[96,6144]{1,0:T(8,128)(2,1)} %bitcast.5), custom_call_target="tpu_custom_call" | custom-call | tf_op jit(solution)/shard_map/pallas_call | solution.py:318
  154.0 1.3 copy.6

commit v3 on v2

--- a/solution.py
+++ b/solution.py
@@ -22,8 +22,8 @@
 
 def kernel(
     tok_ref, gain_ref, w_hbm, wo_hbm, out_ref,
-    x, wraw, wp, wo, stage, acc, ssq, att, part, rsb, slab, fin, ini_s, ini_r,
-    wsem, ini_ss, ini_rs, wo_ss, wo_rs, wo_ls, st_ss, st_rs, zi_ss, z_ss, z_rs, y_ss, y_rs, r_rs,
+    x, wraw, wp, wo, lent, moved, acc, ssq, att, part, rsb, slab, fin, ini_s, ini_r,
+    wsem, ini_ss, ini_rs, wo_ss, wo_rs, wo_ls, near, far, ahead, l_rs, m_ss, m_rs, zi_ss, z_ss, z_rs, y_ss, y_rs, r_rs,
     d_ss, d_rs, a_ss, a_rs, p_ss, p_rs, f_ss, f_rs,
 ):
     s = lax.axis_index("section")
@@ -57,30 +57,15 @@
 
     barrier = pltpu.get_barrier_semaphore()
 
-    def greet(dev):
-        pl.semaphore_signal(barrier, inc=1, device_id=dev, device_id_type=MESH)
+    def signal(sem, dev):
+        pl.semaphore_signal(sem, inc=1, device_id=dev, device_id_type=MESH)
 
     for k in range(1, G):
-        greet(at(s, z, other(j, k)))
-    for k in range(1, Z):
-        greet(at(s, (z + k) % Z, j))
-
-    @pl.when(s < LAST)
-    def _():
-        for k in range(Z):
-            greet(at(s + 1, k, j))
-        for k in range(2):
-            greet(at(LAST, z, 2 * s + k))
-
-    @pl.when(s > 0)
-    def _():
-        for k in range(Z):
-            greet(at(s - 1, k, j))
-
-    @pl.when(jnp.logical_and(s == LAST, y < LAST))
-    def _():
-        for k in range(G):
-            greet(at(y, z, k))
+        signal(barrier, at(s, z, other(j, k)))
+    for k in (1, Z - 1):
+        signal(barrier, at(s, (z + k) % Z, j))
+    for k in (1, LAST):
+        signal(barrier, at((s + k) % (LAST + 1), z, j))
 
     wcopy.wait()
 
@@ -100,8 +85,7 @@
             for m in range(2):
                 ini_s[g, m] = tok_ref[m, :, g * WIDE:(g + 1) * WIDE].astype(F32)
 
-    greeted = G - 1 + Z - 1 + jnp.where(s < LAST, Z + 2, 0) + jnp.where(s > 0, Z, 0)
-    pl.semaphore_wait(barrier, greeted + jnp.where(jnp.logical_and(s == LAST, y < LAST), G, 0))
+    pl.semaphore_wait(barrier, G - 1 + 4)
 
     @pl.when(s == 0)
     def _():
@@ -109,28 +93,55 @@
             to = other(j, k)
             send(ini_s.at[to], ini_r.at[j], ini_ss, ini_rs, at(s, z, to))
 
-    def share_wo(dy, cc, to=None, dst=None, rsem=None):
+    for k in (1, Z - 1):
+        signal(near, at(s, (z + k) % Z, j))
+
+    def columns(goal):
+        return pl.ds(pl.multiple_of(goal * WIDE, WIDE), WIDE)
+
+    def share_wo(dy, cc):
         goal = (y + dy) % Y * 2 + cc
-        columns = pl.ds(pl.multiple_of(goal * WIDE, WIDE), WIDE)
-        if to is None:
-            to, dst, rsem = goal, wo.at[j], wo_rs
-        send(wo_hbm.at[:, columns], dst, wo_ss, rsem, at(s, z, to))
-
-    share_wo(2, 1 - c, other(j, 6), stage, st_rs)
+        send(wo_hbm.at[:, columns(goal)], wo.at[j], wo_ss, wo_rs, at(s, z, goal))
+
+    def lend_wo(dy, cc, sec, i):
+        goal = (y + dy) % Y * 2 + cc
+        send(wo_hbm.at[:, columns(goal)], lent.at[i], wo_ss, l_rs.at[i], at(sec, z, j))
+
     share_wo(0, 1 - c)
-    share_wo(1, c)
-    share_wo(3, c)
-
-    def share_wo_rest():
-        share_wo(2, c)
-        share_wo(1, 1 - c)
-        share_wo(3, 1 - c)
-        drain(stage, st_rs)
-        send(stage, wo.at[other(j, 2)], st_ss, wo_rs, at(s, z, other(j, 6) + 1 - 2 * c))
+
+    @pl.when(s == 0)
+    def _():
+        share_wo(1, c)
+        share_wo(3, c)
+        lend_wo(2, c, LAST, 0)
+        lend_wo(1, 1 - c, 1, 0)
+        lend_wo(2, 1 - c, LAST, 1)
+        lend_wo(3, 1 - c, 1, 1)
+
+    pl.semaphore_wait(near, 2)
+    for k in (2, Z - 2):
+        signal(far, at(s, (z + k) % Z, j))
+    pl.semaphore_wait(far, 2)
 
     @pl.when(s > 0)
     def _():
-        share_wo_rest()
+        signal(ahead, at(s - 1, z, j))
+
+        @pl.when(s != 2)
+        def _():
+            for i in range(2):
+                dy = jnp.where(s == 1, 1 + 2 * i, 2)
+                cc = jnp.where(s == 1, 1 - c, c + i * (1 - 2 * c))
+                drain(lent.at[i], l_rs.at[i])
+                send(lent.at[i], moved.at[i], m_ss, m_rs.at[i], at(s, z, (y + dy) % Y * 2 + cc))
+            for i in range(2):
+                dy = jnp.where(s == 1, 1 + 2 * i, 2)
+                cc = jnp.where(s == 1, 1 - c, c + i * (1 - 2 * c))
+                drain(moved.at[i], m_rs.at[i])
+                send(moved.at[i], wo.at[(y + Y - dy) % Y * 2 + cc], m_ss, wo_rs, at(0, z, j))
+
+        for dy, cc in ((2, c), (1, c), (3, c), (2, 1 - c), (1, 1 - c), (3, 1 - c)):
+            share_wo(dy, cc)
 
     def spread(src, m, sec, ssem, skip_own):
         for d in ORDER:
@@ -219,7 +230,7 @@
         weights = (e / jnp.sum(e, axis=-1, keepdims=True)).astype(BF)
         across = lax.dot_general(v, weights, (((0,), (1,)), ((), ())), preferred_element_type=F32)
         att[m, j] = across[:HEAD].astype(BF)
-        for k in (4, 2, 6, 3, 5, 1, 7):
+        for k in (2, 6, 3, 5, 4, 1, 7):
             send(att.at[m, j], att.at[m, j], a_ss.at[m], a_rs.at[m], at(s, z, other(j, k)))
 
     def project(m):
@@ -239,6 +250,8 @@
 
         @pl.when(s < LAST)
         def _():
+            if m == 0:
+                pl.semaphore_wait(ahead, 1)
             slab[2 + m] = total.astype(BF)
             spread(slab.at[2 + m], m, s + 1, z_ss.at[m], False)
 
@@ -261,10 +274,6 @@
                     send(fin.at[m, to], out_ref.at[m, :, columns], f_ss.at[m], f_rs.at[m, c], at(s, z, to))
 
     take_rows(0)
-
-    @pl.when(s == 0)
-    def _():
-        share_wo_rest()
 
     take_groups(0)
     attend(0)
@@ -279,7 +288,11 @@
     finish(1)
 
     drain(wo.at[pl.ds(0, G - 1)], wo_ss)
-    drain(stage, st_ss)
+
+    @pl.when(jnp.logical_or(s == 1, s == LAST))
+    def _():
+        drain(wo.at[pl.ds(0, 4)], m_ss)
+
 
     @pl.when(s == 0)
     def _():
@@ -314,7 +327,7 @@
 def per_device(video_tokens, norm_gain, qkv_weight, out_weight):
     vmem = pl.BlockSpec(memory_space=pltpu.VMEM)
     anywhere = pl.BlockSpec(memory_space=pl.ANY)
-    dma = pltpu.SemaphoreType.DMA
+    dma, regular = pltpu.SemaphoreType.DMA, pltpu.SemaphoreType.REGULAR
     return pl.pallas_call(
         kernel,
         out_shape=jax.ShapeDtypeStruct((2, 2, 2 * WIDE), F32),
@@ -325,7 +338,8 @@
             pltpu.VMEM((3 * HEAD, D), BF),
             pltpu.VMEM((G, WIDE, 3 * PAD), BF),
             pltpu.VMEM((G, HEAD, WIDE), BF),
-            pltpu.VMEM((HEAD, WIDE), BF),
+            pltpu.VMEM((2, HEAD, WIDE), BF),
+            pltpu.VMEM((2, HEAD, WIDE), BF),
             pltpu.VMEM((2, TOKENS, 3 * PAD), F32),
             pltpu.VMEM((2, TOKENS, 128), F32),
             pltpu.VMEM((2, G, HEAD, TOKENS), BF),
@@ -335,7 +349,8 @@
             pltpu.VMEM((2, G, 2, WIDE), F32),
             pltpu.VMEM((G, 2, 2, WIDE), F32),
             pltpu.VMEM((G, 2, 2, WIDE), F32),
-            dma, dma, dma, dma, dma, dma, dma, dma, dma((2,)), dma((2,)), dma((2, Z)), dma((2,)), dma((2, 2, 2)),
+            dma, dma, dma, dma, dma, dma, regular, regular, regular, dma((2,)), dma, dma((2,)),
+            dma((2,)), dma((2,)), dma((2, Z)), dma((2,)), dma((2, 2, 2)),
             dma((2, 2)), dma((2,)), dma((2, 4)), dma((2,)), dma((2,)), dma((2,)), dma((2,)),
             dma((2,)), dma((2, 2)),
         ],

time: 156 us -> 150 us (0.962)
  Pallas kernels: 154 us -> 149 us
    pallas_call x1, Pallas kernels: 154 us -> 149 us  [per_device(): pl.pallas_call(kernel, out_shape=jax.ShapeDtypeStruct((2, 2, 2 * WIDE), F...]
where the time goes in v3:
time: 150 us
  Pallas kernels  149 us (99%)
    pallas_call x1, Pallas kernels, per_device(): pl.pallas_call(kernel, out_shape=jax.ShapeDtypeStruct((2, 2, 2 * WIDE), F...  149 us

profile of v3, /device:TPU:1, one launch (start us, length us, event | category | flops | bytes accessed | tf_op | source)
XLA Modules:
  0.0 149.9 jit_solution(4415480076334636253)
XLA Ops:
  0.0 148.6 %shard_map.46 = f32[2,2,1536]{2,1,0:T(2,128)} custom-call(bf16[2,2,6144]{2,1,0:T(2,128)(2,1)} %tok_ref.1, f32[1,6144]{1,0:T(1,128)} %gain_ref.1, bf16[288,6144]{1,0:T(8,128)(2,1)} %bitcast.4, bf16[96,6144]{1,0:T(8,128)(2,1)} %bitcast.5), custom_call_target="tpu_custom_call" | custom-call | tf_op jit(solution)/shard_map/pallas_call | solution.py:331
  148.6 1.3 copy.6

commit v4 on v3

--- a/solution.py
+++ b/solution.py
@@ -21,9 +21,9 @@
 
 
 def kernel(
-    tok_ref, gain_ref, w_hbm, wo_hbm, out_ref,
-    x, wraw, wp, wo, lent, moved, acc, ssq, att, part, rsb, slab, fin, ini_s, ini_r,
-    wsem, ini_ss, ini_rs, wo_ss, wo_rs, wo_ls, near, far, ahead, l_rs, m_ss, m_rs, zi_ss, z_ss, z_rs, y_ss, y_rs, r_rs,
+    tok_hbm, gain_hbm, w_hbm, wo_hbm, out_ref,
+    tok_ref, gain_ref, x, wraw, wp, wo, lent, moved, acc, ssq, att, part, rsb, slab, fin, ini_s, ini_r,
+    tsem, gsem, wsem, ini_ss, ini_rs, wo_ss, wo_rs, wo_ls, near, far, ahead, l_rs, m_ss, m_rs, zi_ss, z_ss, z_rs, y_ss, y_rs, r_rs,
     d_ss, d_rs, a_ss, a_rs, p_ss, p_rs, f_ss, f_rs,
 ):
     s = lax.axis_index("section")
@@ -50,6 +50,10 @@
 
     wcopy = pltpu.make_async_copy(w_hbm, wraw, wsem)
     wcopy.start()
+    gcopy = pltpu.make_async_copy(gain_hbm, gain_ref, gsem)
+    gcopy.start()
+    tcopy = pltpu.make_async_copy(tok_hbm, tok_ref, tsem)
+    tcopy.start()
     own_wo = pltpu.make_async_copy(
         wo_hbm.at[:, pl.ds(pl.multiple_of(j * WIDE, WIDE), WIDE)], wo.at[j], wo_ls
     )
@@ -67,6 +71,48 @@
     for k in (1, LAST):
         signal(barrier, at((s + k) % (LAST + 1), z, j))
 
+    tcopy.wait()
+
+    @pl.when(s == 0)
+    def _():
+        for g in range(G):
+            for m in range(2):
+                ini_s[g, m] = tok_ref[m, :, g * WIDE:(g + 1) * WIDE].astype(F32)
+
+    pl.semaphore_wait(barrier, G - 1 + 4)
+
+    @pl.when(s == 0)
+    def _():
+        for k in range(1, G):
+            to = other(j, k)
+            send(ini_s.at[to], ini_r.at[j], ini_ss, ini_rs, at(s, z, to))
+
+    for k in (1, Z - 1):
+        signal(near, at(s, (z + k) % Z, j))
+
+    def columns(goal):
+        return pl.ds(pl.multiple_of(goal * WIDE, WIDE), WIDE)
+
+    def share_wo(dy, cc):
+        goal = (y + dy) % Y * 2 + cc
+        send(wo_hbm.at[:, columns(goal)], wo.at[j], wo_ss, wo_rs, at(s, z, goal))
+
+    def lend_wo(dy, cc, sec, i):
+        goal = (y + dy) % Y * 2 + cc
+        send(wo_hbm.at[:, columns(goal)], lent.at[i], wo_ss, l_rs.at[i], at(sec, z, j))
+
+    share_wo(0, 1 - c)
+
+    @pl.when(s == 0)
+    def _():
+        share_wo(1, c)
+        share_wo(3, c)
+        lend_wo(2, c, LAST, 0)
+        lend_wo(1, 1 - c, 1, 0)
+        lend_wo(2, 1 - c, LAST, 1)
+        lend_wo(3, 1 - c, 1, 1)
+
+    gcopy.wait()
     wcopy.wait()
 
     def prepare(g, carry):
@@ -78,45 +124,6 @@
         return carry
 
     lax.fori_loop(0, G, prepare, 0)
-
-    @pl.when(s == 0)
-    def _():
-        for g in range(G):
-            for m in range(2):
-                ini_s[g, m] = tok_ref[m, :, g * WIDE:(g + 1) * WIDE].astype(F32)
-
-    pl.semaphore_wait(barrier, G - 1 + 4)
-
-    @pl.when(s == 0)
-    def _():
-        for k in range(1, G):
-            to = other(j, k)
-            send(ini_s.at[to], ini_r.at[j], ini_ss, ini_rs, at(s, z, to))
-
-    for k in (1, Z - 1):
-        signal(near, at(s, (z + k) % Z, j))
-
-    def columns(goal):
-        return pl.ds(pl.multiple_of(goal * WIDE, WIDE), WIDE)
-
-    def share_wo(dy, cc):
-        goal = (y + dy) % Y * 2 + cc
-        send(wo_hbm.at[:, columns(goal)], wo.at[j], wo_ss, wo_rs, at(s, z, goal))
-
-    def lend_wo(dy, cc, sec, i):
-        goal = (y + dy) % Y * 2 + cc
-        send(wo_hbm.at[:, columns(goal)], lent.at[i], wo_ss, l_rs.at[i], at(sec, z, j))
-
-    share_wo(0, 1 - c)
-
-    @pl.when(s == 0)
-    def _():
-        share_wo(1, c)
-        share_wo(3, c)
-        lend_wo(2, c, LAST, 0)
-        lend_wo(1, 1 - c, 1, 0)
-        lend_wo(2, 1 - c, LAST, 1)
-        lend_wo(3, 1 - c, 1, 1)
 
     pl.semaphore_wait(near, 2)
     for k in (2, Z - 2):
@@ -170,9 +177,9 @@
             else:
                 drain(chunk, z_rs.at[m, zz])
             half = 0 if i < 4 else 1
+            send(chunk, chunk, y_ss.at[m], r_rs.at[m, half], at(s, z, other(j, 4)))
             send(chunk, chunk, y_ss.at[m], y_rs.at[m, 0, half], at(s, z, other(j, 2)))
             send(chunk, chunk, y_ss.at[m], y_rs.at[m, 1, half], at(s, z, other(j, 6)))
-            send(chunk, chunk, y_ss.at[m], r_rs.at[m, half], at(s, z, other(j, 4)))
         share(m, 0, j)
 
     def sibling(jj):
@@ -203,18 +210,23 @@
         for half in range(2):
             drain(x.at[m, after, half_rows], y_rs.at[m, 1, half])
         share(m, 1, after)
+        multiply(m, after)
         for half in range(2):
             drain(x.at[m, before, half_rows], y_rs.at[m, 0, half])
         share(m, 2, before)
+        drain(x.at[m, j], d_rs.at[m, 0])
+        multiply(m, sibling(j))
+        multiply(m, before)
         for half in range(2):
             drain(x.at[m, across, half_rows], r_rs.at[m, half])
         share(m, 3, across)
-        multiply(m, after)
-        multiply(m, before)
+        drain(x.at[m, after], d_rs.at[m, 1])
+        multiply(m, sibling(after))
         multiply(m, across)
-        for slot, jj in ((0, j), (1, after), (2, before), (3, across)):
-            drain(x.at[m, jj], d_rs.at[m, slot])
-            multiply(m, sibling(jj))
+        drain(x.at[m, before], d_rs.at[m, 2])
+        multiply(m, sibling(before))
+        drain(x.at[m, across], d_rs.at[m, 3])
+        multiply(m, sibling(across))
 
     def attend(m):
         mean = jnp.sum(ssq[m], axis=-1, keepdims=True) * (1.0 / D)
@@ -330,10 +342,12 @@
     dma, regular = pltpu.SemaphoreType.DMA, pltpu.SemaphoreType.REGULAR
     return pl.pallas_call(
         kernel,
-        out_shape=jax.ShapeDtypeStruct((2, 2, 2 * WIDE), F32),
-        in_specs=[vmem, vmem, anywhere, anywhere],
+        out_shape=pltpu.VMEM((2, 2, 2 * WIDE), F32),
+        in_specs=[anywhere] * 4,
         out_specs=vmem,
         scratch_shapes=[
+            pltpu.VMEM((2, 2, D), BF),
+            pltpu.VMEM((1, D), F32),
             pltpu.VMEM((2, G, TOKENS, WIDE), BF),
             pltpu.VMEM((3 * HEAD, D), BF),
             pltpu.VMEM((G, WIDE, 3 * PAD), BF),
@@ -349,7 +363,7 @@
             pltpu.VMEM((2, G, 2, WIDE), F32),
             pltpu.VMEM((G, 2, 2, WIDE), F32),
             pltpu.VMEM((G, 2, 2, WIDE), F32),
-            dma, dma, dma, dma, dma, dma, regular, regular, regular, dma((2,)), dma, dma((2,)),
+            dma, dma, dma, dma, dma, dma, dma, dma, regular, regular, regular, dma((2,)), dma, dma((2,)),
             dma((2,)), dma((2,)), dma((2, Z)), dma((2,)), dma((2, 2, 2)),
             dma((2, 2)), dma((2,)), dma((2, 4)), dma((2,)), dma((2,)), dma((2,)), dma((2,)),
             dma((2,)), dma((2, 2)),

time: 150 us -> 147 us (0.980)
  Pallas kernels: 149 us -> 146 us
    pallas_call x1, Pallas kernels: 149 us -> 146 us  [per_device(): pl.pallas_call(kernel, out_shape=pltpu.VMEM((2, 2, 2 * WIDE), F32), in_sp...]
where the time goes in v4:
time: 147 us
  Pallas kernels  146 us (99%)
    pallas_call x1, Pallas kernels, per_device(): pl.pallas_call(kernel, out_shape=pltpu.VMEM((2, 2, 2 * WIDE), F32), in_sp...  146 us

profile of v4, /device:TPU:1, one launch (start us, length us, event | category | flops | bytes accessed | tf_op | source)
XLA Modules:
  0.0 146.5 jit_solution(11961344943110187558)
XLA Ops:
  0.0 145.9 %shard_map.46 = f32[2,2,1536]{2,1,0:T(2,128)S(1)} custom-call(bf16[2,2,6144]{2,1,0:T(2,128)(2,1)} %tok_hbm.1, f32[1,6144]{1,0:T(1,128)} %gain_hbm.1, bf16[288,6144]{1,0:T(8,128)(2,1)} %bitcast.4, bf16[96,6144]{1,0:T(8,128)(2,1)} %bitcast.5), custom_call_target="tpu_custom_call" | custom-call | tf_op jit(solution)/shard_map/pallas_call | solution.py:343
  145.9 0.6 copy.6
